TPU v7x, 256 devices: a whole 4x4x8 slice. The times are simulated.
256 devices in a mesh: energy: 64 (over y, x_lo, z), layer: 4 (over x_hi, core).
Axes of the slice: x: 4 (x_hi: 2, x_lo: 2; x = x_hi * 2 + x_lo), y: 4, z: 8, core: 2. Of those that a mesh axis runs over, the one named last changes fastest.
Arguments:
- layer_inverse: float32 [64, 32, 256, 256], P('energy', 'layer'), may hold values from -0.008125 to 1, as said below
- coupling: float32 [256, 256], replicated, may hold values from -0.5125 to 0.5125, as said below
- lead_left: float32 [64, 256, 256], P('energy'), may hold values from -0.0040625 to 0.5, as said below
- lead_right: float32 [64, 256, 256], P('energy'), may hold values from -0.0040625 to 0.5, as said below
- quad_weight: float32 [64], replicated, may hold values from 0.0015625 to 0.0625
- energy_slot: int32 [64], P('energy'), may hold values from 0 to 63, each once
- plane_of: int32 [32], replicated, may hold values from 0 to 1023
- doping: float32 [1024, 128, 128], P(('energy', 'layer')), may hold values from -6 to 6
- screening: float32 [1024, 128, 128], P(('energy', 'layer')), may hold values from 0.25 to 2
Outputs:
- layer_density: float32 [32, 256], P('layer')
- potential: float32 [1024, 128, 128], P(('energy', 'layer'))
- residual: float32 [1024, 128, 128], P(('energy', 'layer'))
Inputs may be any that keep to these rules, and one draw needn't show every extreme that they name: `layer_inverse`: each block is symmetric; its diagonal entries lie between 0.3 and 1.0 and its other entries within 0.13 * 256 ** -0.5 of zero. `coupling`: entries are independent with mean zero. `lead_left`: each block is symmetric; its diagonal entries lie between 0.15 and 0.5 and its other entries within 0.065 * 256 ** -0.5 of zero. `lead_right`: each block is symmetric; its diagonal entries lie between 0.15 and 0.5 and its other entries within 0.065 * 256 ** -0.5 of zero. `energy_slot`: every quadrature index appears once. `plane_of`: several layers may share a plane.
All inputs are finite; a program needn't handle non-finite values.
Results may differ from a plain program's by a relative error of at most 0.00018.
Values sent between devices are 32-bit elements; how exact they have to be, the bound alone decides.
A program may use at most 128 MiB of HBM per device.

v0:
```python
import functools

import jax
import jax.numpy as jnp
from jax import lax
from jax.experimental import pallas as pl
from jax.experimental.pallas import tpu as pltpu
from jax.sharding import Mesh
from jax.sharding import PartitionSpec as P

AXES = ("energy_0", "energy_1", "energy_2", "layer_0", "layer_1")
LAYER = ("layer_0", "layer_1")
ENERGY = ("energy_0", "energy_1", "energy_2")
ORB = 16
CG_ITERS = 3
SHIFT = 7.0
PIECES = 2
MESH = pl.DeviceIdType.MESH
HI = lax.Precision.HIGHEST
F32 = jnp.float32
BF16 = jnp.bfloat16


def parts_of(x, count):
    parts = []
    for _ in range(count):
        part = x.astype(BF16)
        parts.append(part)
        x = x - part.astype(F32)
    return parts


def mm(left, right):
    total = None
    most = max(len(left), len(right))
    for i, a in enumerate(left):
        for j, b in enumerate(right):
            if i + j < most:
                term = jnp.dot(a, b, preferred_element_type=F32)
                total = term if total is None else total + term
    return total


def kernel(
    sizes,
    inv_hbm, t_ref, lead_l, lead_r, qw_ref, slot_ref, plane_ref, dop_hbm, scr_hbm,
    dens_out, pot_out, res_out,
    inv, tb, ttb, s_l, s_r, k_l, k_r, acc, e_l, e_r, out_l, out_r,
    dopx, scrx, u1, u2, u3, part, zbuf, pbuf, psrc, mom, zmom, pmom, msrc,
    inv_sem, own_sem, halo_send, halo_recv, relay_send, relay_recv,
    zs, zr, ps, pr, mzs, mzr, mps, mpr,
):
    ny, nxl, nz, nxh, nc = sizes
    y, xl, z, xh, c = [lax.axis_index(a) for a in AXES]
    n_layer = nxh * nc
    n_plane = ny * nxl * n_layer
    n_energy = ny * nxl * nz
    layer = xh * nc + c
    energy = (y * nxl + xl) * nz + z
    slab = energy * n_layer + layer
    n_slabs = n_energy * n_layer
    here = (y * nxl + xl) * n_layer + layer
    count, size, _ = inv_hbm.shape
    planes = dop_hbm.shape[0]

    def plane_dev(index):
        group, lay = lax.div(index, n_layer), lax.rem(index, n_layer)
        return (lax.div(group, nxl), lax.rem(group, nxl), z, lax.div(lay, nc), lax.rem(lay, nc))

    def z_dev(index):
        return (y, xl, index, xh, c)

    def slab_dev(index):
        en, lay = lax.div(index, n_layer), lax.rem(index, n_layer)
        group, zz = lax.div(en, nz), lax.rem(en, nz)
        return (lax.div(group, nxl), lax.rem(group, nxl), zz, lax.div(lay, nc), lax.rem(lay, nc))

    barrier = pltpu.get_barrier_semaphore()
    extra_up = jnp.logical_and(layer == n_layer - 1, energy < n_energy - 1)
    extra_down = jnp.logical_and(layer == 0, energy > 0)
    for k in range(1, nz):
        pl.semaphore_signal(barrier, inc=1, device_id=z_dev(lax.rem(z + k, nz)), device_id_type=MESH)
    for k in range(1, n_plane):
        pl.semaphore_signal(barrier, inc=1, device_id=plane_dev(lax.rem(here + k, n_plane)), device_id_type=MESH)

    @pl.when(extra_up)
    def _():
        pl.semaphore_signal(barrier, inc=1, device_id=slab_dev(slab + 1), device_id_type=MESH)

    @pl.when(extra_down)
    def _():
        pl.semaphore_signal(barrier, inc=1, device_id=slab_dev(slab - 1), device_id_type=MESH)

    loads = []
    for i in range(count // 2):
        for l in (i, count - 1 - i):
            loads.append(pltpu.make_async_copy(inv_hbm.at[l], inv.at[l], inv_sem.at[l]))
    own = [
        pltpu.make_async_copy(dop_hbm, dopx.at[pl.ds(3, planes)], own_sem.at[0]),
        pltpu.make_async_copy(scr_hbm, scrx.at[pl.ds(2, planes)], own_sem.at[1]),
    ]
    for copy in loads + own:
        copy.start()

    t = t_ref[...]
    for n, (piece, across) in enumerate(zip(parts_of(t, PIECES), parts_of(t.T, PIECES))):
        tb[n] = piece
        ttb[n] = across

    rows = lax.broadcasted_iota(jnp.int32, (size, size), 0)
    cols = lax.broadcasted_iota(jnp.int32, (size, size), 1)

    def diagonal(mat):
        return jnp.sum(jnp.where(rows == cols, mat, 0.0), axis=0, keepdims=True)

    def propagators(l, left):
        d = parts_of(inv[l], PIECES)
        a, b = (tb, ttb) if left else (ttb, tb)
        a, b = [a[n] for n in range(PIECES)], [b[n] for n in range(PIECES)]
        return mm(d, a), mm(b, d)

    def first(left):
        l = 0 if left else count - 1
        s, k = (s_l, k_l) if left else (s_r, k_r)
        _, pt = propagators(l, left)
        s[...] = inv[l]
        k[l] = pt
        acc[l : l + 1, :] = jnp.zeros((1, size), F32)

    def step(i, left):
        l = i if left else count - 1 - i
        before = i - 1 if left else count - i
        s, k = (s_l, k_l) if left else (s_r, k_r)
        p, pt = propagators(l, left)
        ptb = parts_of(pt, PIECES)
        y_mat = mm(parts_of(s[...], PIECES), ptb)
        k[l] = mm(parts_of(k[before], PIECES), ptb)
        moved = mm(parts_of(p, PIECES), parts_of(y_mat, PIECES))
        new = inv[l] + moved
        s[...] = new
        return l, diagonal(moved)

    loads[0].wait()
    loads[1].wait()
    first(True)
    first(False)
    for copy in loads[2:]:
        copy.wait()
    for i in range(count):
        acc[i : i + 1, :] = diagonal(inv[i])

    def both(i, carry):
        for left in (True, False):
            l, row = step(i, left)
            acc[pl.ds(l, 1), :] = acc[pl.ds(l, 1), :] + row
        return carry

    lax.fori_loop(1, count, both, 0)

    more = jnp.where(extra_up, 1, 0) + jnp.where(extra_down, 1, 0)
    pl.semaphore_wait(barrier, nz - 1 + n_plane - 1 + more)

    def halo_up():
        dev = slab_dev(slab + 1)
        return [
            pltpu.make_async_remote_copy(
                dop_hbm.at[pl.ds(planes - 3, 3)], dopx.at[pl.ds(0, 3)],
                halo_send.at[0], halo_recv.at[0], device_id=dev, device_id_type=MESH),
            pltpu.make_async_remote_copy(
                scr_hbm.at[pl.ds(planes - 2, 2)], scrx.at[pl.ds(0, 2)],
                halo_send.at[1], halo_recv.at[1], device_id=dev, device_id_type=MESH),
        ]

    def halo_down():
        dev = slab_dev(slab - 1)
        return [
            pltpu.make_async_remote_copy(
                dop_hbm.at[pl.ds(0, 3)], dopx.at[pl.ds(planes + 3, 3)],
                halo_send.at[2], halo_recv.at[2], device_id=dev, device_id_type=MESH),
            pltpu.make_async_remote_copy(
                scr_hbm.at[pl.ds(0, 2)], scrx.at[pl.ds(planes + 2, 2)],
                halo_send.at[3], halo_recv.at[3], device_id=dev, device_id_type=MESH),
        ]

    has_up = slab < n_slabs - 1
    has_down = slab > 0

    @pl.when(has_up)
    def _():
        for copy in halo_up():
            copy.start()

    @pl.when(has_down)
    def _():
        for copy in halo_down():
            copy.start()

    def relay(left):
        out, e = (out_l, e_l) if left else (out_r, e_r)
        n = 0 if left else 1
        to = layer + 1 if left else layer - 1
        dev = plane_dev((y * nxl + xl) * n_layer + to)
        return pltpu.make_async_remote_copy(
            out, e, relay_send.at[n], relay_recv.at[n], device_id=dev, device_id_type=MESH
        )

    def enter(left):
        s, k, e, out = (s_l, k_l, e_l, out_l) if left else (s_r, k_r, e_r, out_r)
        lead = lead_l if left else lead_r
        at_edge = layer == (0 if left else n_layer - 1)
        at_end = layer == (n_layer - 1 if left else 0)

        @pl.when(at_edge)
        def _():
            e[...] = lead[...]

        @pl.when(jnp.logical_not(at_edge))
        def _():
            relay(left).wait_recv()

        eb = parts_of(e[...], PIECES)
        last = count - 1 if left else 0
        k_last = k[last]
        g = mm(eb, parts_of(k_last, PIECES))
        acc[last : last + 1, :] = acc[last : last + 1, :] + jnp.sum(g * k_last, axis=0, keepdims=True)

        @pl.when(jnp.logical_not(at_end))
        def _():
            out[...] = s[...] + mm(parts_of(k_last.T, PIECES), parts_of(g, PIECES))
            relay(left).start()

        for i in range(1, count):
            l = count - 1 - i if left else i
            k_here = k[l]
            g = mm(eb, parts_of(k_here, PIECES))
            acc[l : l + 1, :] = acc[l : l + 1, :] + jnp.sum(g * k_here, axis=0, keepdims=True)

    @pl.when(layer < n_layer // 2)
    def _():
        enter(True)
        enter(False)

    @pl.when(layer >= n_layer // 2)
    def _():
        enter(False)
        enter(True)

    slots = lax.broadcasted_iota(jnp.int32, qw_ref.shape, 1)
    weight = jnp.sum(jnp.where(slots == slot_ref[0], qw_ref[...], 0.0), axis=1, keepdims=True)
    part[...] = weight * acc[...]

    def z_copies(src, buf, send, recv):
        done = []
        for k in range(1, nz):
            to = lax.rem(z + k, nz)
            done.append(pltpu.make_async_remote_copy(
                src, buf.at[z], send.at[to], recv.at[z], device_id=z_dev(to), device_id_type=MESH))
        return done

    def z_arrivals(src, buf, send, recv):
        done = []
        for k in range(1, nz):
            source = lax.rem(z + k, nz)
            done.append(pltpu.make_async_remote_copy(
                src, buf.at[source], send.at[source], recv.at[source], device_id=z_dev(source), device_id_type=MESH))
        return done

    def p_copies(src, buf, send, recv):
        done = []
        for k in range(1, n_plane):
            to = lax.rem(here + k, n_plane)
            done.append(pltpu.make_async_remote_copy(
                src, buf.at[here], send.at[to], recv.at[here], device_id=plane_dev(to), device_id_type=MESH))
        return done

    def p_arrivals(src, buf, send, recv):
        done = []
        for k in range(1, n_plane):
            source = lax.rem(here + k, n_plane)
            done.append(pltpu.make_async_remote_copy(
                src, buf.at[source], send.at[source], recv.at[source], device_id=plane_dev(source), device_id_type=MESH))
        return done

    def exchange(copies, arrivals, src, buf, mine, send, recv):
        for copy in copies(src, buf, send, recv):
            copy.start()
        buf[mine] = src[...]
        for copy in arrivals(src, buf, send, recv):
            copy.wait_recv()

    exchange(z_copies, z_arrivals, part, zbuf, z, zs, zr)
    total = zbuf[0]
    for k in range(1, nz):
        total = total + zbuf[k]
    psrc[...] = total
    exchange(p_copies, p_arrivals, psrc, pbuf, here, ps, pr)
    gathered = []
    for lay in range(n_layer):
        total = pbuf[lay]
        for k in range(1, ny * nxl):
            total = total + pbuf[k * n_layer + lay]
        gathered.append(total)
    dens = jnp.concatenate(gathered, axis=0)
    mine = gathered[0]
    for lay in range(1, n_layer):
        mine = jnp.where(layer == lay, gathered[lay], mine)
    dens_out[...] = mine

    for copy in own:
        copy.wait()

    @pl.when(has_down)
    def _():
        for copy in halo_up():
            copy.wait_recv()

    @pl.when(has_up)
    def _():
        for copy in halo_down():
            copy.wait_recv()

    @pl.when(jnp.logical_not(has_down))
    def _():
        dopx[0:3] = jnp.zeros((3, *dopx.shape[1:]), F32)
        scrx[0:2] = jnp.zeros((2, *scrx.shape[1:]), F32)

    @pl.when(jnp.logical_not(has_up))
    def _():
        dopx[planes + 3 : planes + 6] = jnp.zeros((3, *dopx.shape[1:]), F32)
        scrx[planes + 2 : planes + 4] = jnp.zeros((2, *scrx.shape[1:]), F32)

    low = slab * planes - 3
    n_near = planes + 6
    near = 16
    ids = low + lax.broadcasted_iota(jnp.int32, (near, plane_ref.shape[1]), 0)
    onehot = jnp.where(plane_ref[...] == ids, 1.0, 0.0)
    pc = jnp.dot(onehot, dens, precision=HI, preferred_element_type=F32)
    n_side = dop_hbm.shape[2]
    cell = n_side // ORB
    spread_m = lax.broadcasted_iota(jnp.int32, (size, n_side), 0)
    spread_z = lax.broadcasted_iota(jnp.int32, (size, n_side), 1)
    spread = jnp.where(lax.rem(spread_m, ORB) == lax.div(spread_z, cell), 1.0, 0.0)
    row_j = lax.broadcasted_iota(jnp.int32, (ORB, size), 0)
    row_m = lax.broadcasted_iota(jnp.int32, (ORB, size), 1)
    own_row = row_j == lax.div(row_m, ORB)
    tall = jnp.concatenate([jnp.where(own_row, pc[q : q + 1, :], 0.0) for q in range(n_near)], axis=0)
    wide = jnp.dot(tall, spread, precision=HI, preferred_element_type=F32)
    n_y = dop_hbm.shape[1]
    for q in range(n_near):
        for j in range(ORB):
            row = wide[q * ORB + j : q * ORB + j + 1, :]
            where = pl.ds(j * (n_y // ORB), n_y // ORB)
            dopx[q, where, :] = row - dopx[q, where, :]

    at_y = lax.broadcasted_iota(jnp.int32, (n_y, n_side), 0)
    at_z = lax.broadcasted_iota(jnp.int32, (n_y, n_side), 1)

    def applied(src, dst, trim):
        n_dst = n_near - 2 * trim
        for q in range(n_dst):
            mid = src[q + 1]
            beside = src[q] + src[q + 2]
            beside = beside + jnp.where(at_y == 0, 0.0, pltpu.roll(mid, 1, 0))
            beside = beside + jnp.where(at_y == n_y - 1, 0.0, pltpu.roll(mid, n_y - 1, 0))
            beside = beside + jnp.where(at_z == 0, 0.0, pltpu.roll(mid, 1, 1))
            beside = beside + jnp.where(at_z == n_side - 1, 0.0, pltpu.roll(mid, n_side - 1, 1))
            value = (scrx[q + trim - 1] + (6.0 - SHIFT)) * mid - beside
            if q < 3 - trim:
                value = jnp.where(has_down, value, 0.0)
            if q >= 3 - trim + planes:
                value = jnp.where(has_up, value, 0.0)
            dst[q] = value

    applied(dopx, u1, 1)
    applied(u1, u2, 2)
    applied(u2, u3, 3)

    def inner(a, a0, b, b0):
        total = None
        for q in range(planes):
            term = a[a0 + q] * b[b0 + q]
            total = term if total is None else total + term
        return jnp.sum(jnp.sum(total, axis=0, keepdims=True), axis=1, keepdims=True)

    sums = [
        inner(dopx, 3, dopx, 3), inner(dopx, 3, u1, 2), inner(u1, 2, u1, 2),
        inner(u1, 2, u2, 1), inner(u2, 1, u2, 1), inner(u2, 1, u3, 0),
    ]
    lane = lax.broadcasted_iota(jnp.int32, (1, 128), 1)
    row = jnp.zeros((1, 128), F32)
    for k, value in enumerate(sums):
        row = jnp.where(lane == k, value, row)
    mom[...] = row
    exchange(z_copies, z_arrivals, mom, zmom, z, mzs, mzr)
    total = zmom[0]
    for k in range(1, nz):
        total = total + zmom[k]
    msrc[...] = total
    exchange(p_copies, p_arrivals, msrc, pmom, here, mps, mpr)
    total = pmom[0]
    for k in range(1, n_plane):
        total = total + pmom[k]
    moment = [total[:, k : k + 1] for k in range(6)]

    def product(a, b):
        value = None
        for i, p in enumerate(a):
            for j, q in enumerate(b):
                term = p * q * moment[i + j]
                value = term if value is None else value + term
        return value

    def times_a(a):
        shifted = [None, *a]
        kept = [SHIFT * v for v in a] + [None]
        return [w if v is None else v if w is None else v + w for v, w in zip(shifted, kept)]

    def plus(a, factor, b):
        longest = max(len(a), len(b))
        result = []
        for i in range(longest):
            if i >= len(b):
                result.append(a[i])
            elif i >= len(a):
                result.append(factor * b[i])
            else:
                result.append(a[i] + factor * b[i])
        return result

    one = jnp.ones((1, 1), F32)
    residual, direction, potential = [one], [one], []
    norm = moment[0]
    for iteration in range(CG_ITERS):
        a_dir = times_a(direction)
        step_size = norm / product(direction, a_dir)
        potential = plus(potential, step_size, direction)
        residual = plus(residual, -step_size, a_dir)
        if iteration + 1 < CG_ITERS:
            new = product(residual, residual)
            direction = plus(residual, new / norm, direction)
            norm = new

    for q in range(planes):
        v = [dopx[3 + q], u1[2 + q], u2[1 + q], u3[q]]
        x = potential[0] * v[0]
        for k in range(1, CG_ITERS):
            x = x + potential[k] * v[k]
        pot_out[q] = x
        r = residual[0] * v[0]
        for k in range(1, CG_ITERS + 1):
            r = r + residual[k] * v[k]
        res_out[q] = r

    for copy in z_copies(part, zbuf, zs, zr) + z_copies(mom, zmom, mzs, mzr):
        copy.wait_send()
    for copy in p_copies(psrc, pbuf, ps, pr) + p_copies(msrc, pmom, mps, mpr):
        copy.wait_send()

    @pl.when(layer < n_layer - 1)
    def _():
        relay(True).wait_send()

    @pl.when(layer > 0)
    def _():
        relay(False).wait_send()

    @pl.when(has_up)
    def _():
        for copy in halo_up():
            copy.wait_send()

    @pl.when(has_down)
    def _():
        for copy in halo_down():
            copy.wait_send()


def body(
    sizes,
    layer_inverse,
    coupling,
    lead_left,
    lead_right,
    quad_weight,
    energy_slot,
    plane_of,
    doping,
    screening,
):
    ny, nxl, nz, nxh, nc = sizes
    _, count, size, _ = layer_inverse.shape
    planes, n_y, n_z = doping.shape
    n_plane = ny * nxl * nxh * nc
    vmem = pl.BlockSpec(memory_space=pltpu.VMEM)
    hbm = pl.BlockSpec(memory_space=pl.ANY)
    smem = pl.BlockSpec(memory_space=pltpu.SMEM)
    square = pltpu.VMEM((size, size), F32)
    squares = pltpu.VMEM((count, size, size), F32)
    dma = pltpu.SemaphoreType.DMA
    rows = pltpu.VMEM((count, size), F32)
    return pl.pallas_call(
        functools.partial(kernel, sizes),
        out_shape=(
            jax.ShapeDtypeStruct((count, size), F32),
            jax.ShapeDtypeStruct(doping.shape, F32),
            jax.ShapeDtypeStruct(doping.shape, F32),
        ),
        in_specs=[hbm, vmem, vmem, vmem, vmem, smem, vmem, hbm, hbm],
        out_specs=(vmem, vmem, vmem),
        scratch_shapes=[
            squares,
            pltpu.VMEM((PIECES, size, size), BF16),
            pltpu.VMEM((PIECES, size, size), BF16),
            square, square, squares, squares, rows, square, square, square, square,
            pltpu.VMEM((planes + 6, n_y, n_z), F32),
            pltpu.VMEM((planes + 4, n_y, n_z), F32),
            pltpu.VMEM((planes + 4, n_y, n_z), F32),
            pltpu.VMEM((planes + 2, n_y, n_z), F32),
            pltpu.VMEM((planes, n_y, n_z), F32),
            rows,
            pltpu.VMEM((nz, count, size), F32),
            pltpu.VMEM((n_plane, count, size), F32),
            rows,
            pltpu.VMEM((1, 128), F32),
            pltpu.VMEM((nz, 1, 128), F32),
            pltpu.VMEM((n_plane, 1, 128), F32),
            pltpu.VMEM((1, 128), F32),
            dma((count,)), dma((2,)), dma((4,)), dma((4,)), dma((2,)), dma((2,)),
            dma((nz,)), dma((nz,)), dma((n_plane,)), dma((n_plane,)),
            dma((nz,)), dma((nz,)), dma((n_plane,)), dma((n_plane,)),
        ],
        compiler_params=pltpu.CompilerParams(
            collective_id=0, has_side_effects=True, vmem_limit_bytes=48 * 1024 * 1024
        ),
    )(
        layer_inverse[0],
        coupling,
        lead_left[0],
        lead_right[0],
        quad_weight[None],
        energy_slot,
        plane_of[None],
        doping,
        screening,
    )


def sharded(split):
    energy_layer = (*ENERGY, *LAYER)
    in_specs = (
        P(ENERGY, LAYER, None, None),
        P(),
        P(ENERGY, None, None),
        P(ENERGY, None, None),
        P(),
        P(ENERGY),
        P(),
        P(energy_layer, None, None),
        P(energy_layer, None, None),
    )
    out_specs = (P(LAYER, None), P(energy_layer, None, None), P(energy_layer, None, None))
    sizes = tuple(split.shape[a] for a in AXES)
    return jax.shard_map(
        functools.partial(body, sizes), mesh=split, in_specs=in_specs, out_specs=out_specs, check_vma=False
    )


def solution(mesh):
    return sharded(Mesh(mesh.devices.reshape(4, 2, 8, 2, 2), AXES))
```

profile of v0, /device:TPU:1, one launch (start us, length us, event | category | flops | bytes accessed | tf_op | source)
XLA Modules:
  0.0 70.6 jit_solution(7150962351085645583)
XLA Ops:
  1.3 0.0 copy-start
  1.3 1.6 %copy-done = f32[1,8,256,256]{3,2,1,0:T(8,128)S(1)} copy-done((f32[1,8,256,256]{3,2,1,0:T(8,128)S(1)}, f32[1,8,256,256]{3,2,1,0:T(8,128)}, u32[]{:S(2)}) %copy-start) | copy-done | bytes 2097176
  2.9 0.0 copy-start.1
  2.9 0.9 %copy-done.1 = f32[256,256]{1,0:T(8,128)S(1)} copy-done((f32[256,256]{1,0:T(8,128)S(1)}, f32[256,256]{1,0:T(8,128)}, u32[]{:S(2)}) %copy-start.1) | copy-done | bytes 262168
  3.8 0.0 copy-start.2
  3.8 0.9 %copy-done.2 = f32[1,256,256]{2,1,0:T(8,128)S(1)} copy-done((f32[1,256,256]{2,1,0:T(8,128)S(1)}, f32[1,256,256]{2,1,0:T(8,128)}, u32[]{:S(2)}) %copy-start.2) | copy-done | bytes 262168
  4.8 0.0 copy-start.3
  4.8 0.9 %copy-done.3 = f32[1,256,256]{2,1,0:T(8,128)S(1)} copy-done((f32[1,256,256]{2,1,0:T(8,128)S(1)}, f32[1,256,256]{2,1,0:T(8,128)}, u32[]{:S(2)}) %copy-start.3) | copy-done | bytes 262168
  5.7 0.0 copy-start.4
  5.7 0.9 %copy-done.4 = f32[4,128,128]{2,1,0:T(8,128)S(1)} copy-done((f32[4,128,128]{2,1,0:T(8,128)S(1)}, f32[4,128,128]{2,1,0:T(8,128)}, u32[]{:S(2)}) %copy-start.4) | copy-done | bytes 262168
  6.7 0.0 copy-start.5
  6.7 0.9 %copy-done.5 = f32[4,128,128]{2,1,0:T(8,128)S(1)} copy-done((f32[4,128,128]{2,1,0:T(8,128)S(1)}, f32[4,128,128]{2,1,0:T(8,128)}, u32[]{:S(2)}) %copy-start.5) | copy-done | bytes 262168
  7.6 0.0 copy-start.6
  7.6 0.7 copy-done.6
  8.3 0.0 copy-start.7
  8.3 0.7 copy-done.7
  8.9 59.6 %shard_map.112 = (f32[8,256]{1,0:T(8,128)S(1)}, f32[4,128,128]{2,1,0:T(8,128)S(1)}, f32[4,128,128]{2,1,0:T(8,128)S(1)}) custom-call(f32[8,256,256]{2,1,0:T(8,128)S(1)} %bitcast.5, f32[256,256]{1,0:T(8,128)S(1)} %copy-done.1, f32[256,256]{1,0:T(8,128)S(1)} %bitcast.6, f32[256,256]{1,0:T(8,128)S(1)} %bitcast.7, f32[1,64]{1,0:T(1,128)S(1)} %bitcast.8, ...), custom_call_target="tpu_custom_call" | custom-call | tf_op jit(solution)/shard_map/pallas_call | solution.py:501
  68.5 0.6 copy.16
  69.1 0.7 copy.17
  69.8 0.7 copy.18
Async XLA Ops:
  1.3 1.6 %copy-start = (f32[1,8,256,256]{3,2,1,0:T(8,128)S(1)}, f32[1,8,256,256]{3,2,1,0:T(8,128)}, u32[]{:S(2)}) copy-start(f32[1,8,256,256]{3,2,1,0:T(8,128)} %param.9) | copy-start | bytes 6291460
  2.9 0.9 %copy-start.1 = (f32[256,256]{1,0:T(8,128)S(1)}, f32[256,256]{1,0:T(8,128)}, u32[]{:S(2)}) copy-start(f32[256,256]{1,0:T(8,128)} %t_ref.1) | copy-start | bytes 786436
  3.8 0.9 %copy-start.2 = (f32[1,256,256]{2,1,0:T(8,128)S(1)}, f32[1,256,256]{2,1,0:T(8,128)}, u32[]{:S(2)}) copy-start(f32[1,256,256]{2,1,0:T(8,128)} %param.11) | copy-start | bytes 786436
  4.8 0.9 %copy-start.3 = (f32[1,256,256]{2,1,0:T(8,128)S(1)}, f32[1,256,256]{2,1,0:T(8,128)}, u32[]{:S(2)}) copy-start(f32[1,256,256]{2,1,0:T(8,128)} %param.12) | copy-start | bytes 786436
  5.7 0.9 %copy-start.4 = (f32[4,128,128]{2,1,0:T(8,128)S(1)}, f32[4,128,128]{2,1,0:T(8,128)}, u32[]{:S(2)}) copy-start(f32[4,128,128]{2,1,0:T(8,128)} %dop_hbm.1) | copy-start | bytes 786436
  6.7 0.9 %copy-start.5 = (f32[4,128,128]{2,1,0:T(8,128)S(1)}, f32[4,128,128]{2,1,0:T(8,128)}, u32[]{:S(2)}) copy-start(f32[4,128,128]{2,1,0:T(8,128)} %scr_hbm.1) | copy-start | bytes 786436
  7.6 0.7 copy-start.6
  8.3 0.7 copy-start.7
where the time goes:
time: 70.8 us; the launch traced here: 70.6 us
  Pallas kernels  59.6 us (84%)
  local copies, waits for them, and re-layouts  9.65 us (14%)
  between operations  1.3 us (2%)
    pallas_call x1, Pallas kernels, body(): pl.pallas_call(functools.partial(kernel, sizes), out_shape=(jax.ShapeDtyp...  59.6 us
    unnamed x19, local copies, waits for them, and re-layouts  9.65 us

commit v1 on v0

--- a/solution.py
+++ b/solution.py
@@ -14,7 +14,13 @@
 ORB = 16
 CG_ITERS = 3
 SHIFT = 7.0
-PIECES = 2
+VMEM = 48 * 1024 * 1024
+PROP = (2, 2)
+PULL = (2, 2)
+CARRY = (2, 2)
+MOVE = (2, 2)
+ENTER = (1, 1)
+LEAVE = (1, 1)
 MESH = pl.DeviceIdType.MESH
 HI = lax.Precision.HIGHEST
 F32 = jnp.float32
@@ -43,9 +49,9 @@
 
 def kernel(
     sizes,
-    inv_hbm, t_ref, lead_l, lead_r, qw_ref, slot_ref, plane_ref, dop_hbm, scr_hbm,
+    inv_hbm, t_hbm, lead_l, lead_r, qw_hbm, slot_hbm, plane_hbm, dop_hbm, scr_hbm,
     dens_out, pot_out, res_out,
-    inv, tb, ttb, s_l, s_r, k_l, k_r, acc, e_l, e_r, out_l, out_r,
+    inv, t_ref, tt, p_b, pt_b, s_ref, k_ref, acc, e_ref, wire_in, wire_out, qw_ref, slot_ref, plane_ref,
     dopx, scrx, u1, u2, u3, part, zbuf, pbuf, psrc, mom, zmom, pmom, msrc,
     inv_sem, own_sem, halo_send, halo_recv, relay_send, relay_recv,
     zs, zr, ps, pr, mzs, mzr, mps, mpr,
@@ -91,21 +97,38 @@
     def _():
         pl.semaphore_signal(barrier, inc=1, device_id=slab_dev(slab - 1), device_id_type=MESH)
 
-    loads = []
-    for i in range(count // 2):
-        for l in (i, count - 1 - i):
-            loads.append(pltpu.make_async_copy(inv_hbm.at[l], inv.at[l], inv_sem.at[l]))
+    first = jnp.where(layer >= n_layer // 2, 1, 0)
+
+    def layer_at(q, i):
+        return q * (count - 1) + (1 - 2 * q) * i
+
+    t_load = pltpu.make_async_copy(t_hbm, t_ref, own_sem.at[2])
+    t_load.start()
+    for i in range(count):
+        l = layer_at(first, i)
+        pltpu.make_async_copy(inv_hbm.at[l], inv.at[l], inv_sem.at[l]).start()
+    lead_loads = [
+        pltpu.make_async_copy(lead_l, e_ref.at[0], own_sem.at[3]),
+        pltpu.make_async_copy(lead_r, e_ref.at[1], own_sem.at[4]),
+    ]
+    edges = [layer == 0, layer == n_layer - 1]
+    for edge, copy in zip(edges, lead_loads):
+        pl.when(edge)(copy.start)
     own = [
         pltpu.make_async_copy(dop_hbm, dopx.at[pl.ds(3, planes)], own_sem.at[0]),
         pltpu.make_async_copy(scr_hbm, scrx.at[pl.ds(2, planes)], own_sem.at[1]),
+        pltpu.make_async_copy(qw_hbm, qw_ref, own_sem.at[5]),
+        pltpu.make_async_copy(slot_hbm, slot_ref, own_sem.at[6]),
+        pltpu.make_async_copy(plane_hbm, plane_ref, own_sem.at[7]),
     ]
-    for copy in loads + own:
+    for copy in own:
         copy.start()
 
+    t_load.wait()
     t = t_ref[...]
-    for n, (piece, across) in enumerate(zip(parts_of(t, PIECES), parts_of(t.T, PIECES))):
-        tb[n] = piece
-        ttb[n] = across
+    for n, (piece, across) in enumerate(zip(parts_of(t, PROP[1]), parts_of(t.T, PROP[1]))):
+        tt[0, n] = piece
+        tt[1, n] = across
 
     rows = lax.broadcasted_iota(jnp.int32, (size, size), 0)
     cols = lax.broadcasted_iota(jnp.int32, (size, size), 1)
@@ -113,52 +136,38 @@
     def diagonal(mat):
         return jnp.sum(jnp.where(rows == cols, mat, 0.0), axis=0, keepdims=True)
 
-    def propagators(l, left):
-        d = parts_of(inv[l], PIECES)
-        a, b = (tb, ttb) if left else (ttb, tb)
-        a, b = [a[n] for n in range(PIECES)], [b[n] for n in range(PIECES)]
+    def propagator(q, i):
+        d = parts_of(inv[layer_at(q, i)], PROP[0])
+        a = [tt[q, n] for n in range(PROP[1])]
+        b = [tt[1 - q, n] for n in range(PROP[1])]
         return mm(d, a), mm(b, d)
 
-    def first(left):
-        l = 0 if left else count - 1
-        s, k = (s_l, k_l) if left else (s_r, k_r)
-        _, pt = propagators(l, left)
-        s[...] = inv[l]
-        k[l] = pt
-        acc[l : l + 1, :] = jnp.zeros((1, size), F32)
-
-    def step(i, left):
-        l = i if left else count - 1 - i
-        before = i - 1 if left else count - i
-        s, k = (s_l, k_l) if left else (s_r, k_r)
-        p, pt = propagators(l, left)
-        ptb = parts_of(pt, PIECES)
-        y_mat = mm(parts_of(s[...], PIECES), ptb)
-        k[l] = mm(parts_of(k[before], PIECES), ptb)
-        moved = mm(parts_of(p, PIECES), parts_of(y_mat, PIECES))
-        new = inv[l] + moved
-        s[...] = new
-        return l, diagonal(moved)
-
-    loads[0].wait()
-    loads[1].wait()
-    first(True)
-    first(False)
-    for copy in loads[2:]:
-        copy.wait()
-    for i in range(count):
-        acc[i : i + 1, :] = diagonal(inv[i])
-
-    def both(i, carry):
-        for left in (True, False):
-            l, row = step(i, left)
-            acc[pl.ds(l, 1), :] = acc[pl.ds(l, 1), :] + row
-        return carry
-
-    lax.fori_loop(1, count, both, 0)
-
-    more = jnp.where(extra_up, 1, 0) + jnp.where(extra_down, 1, 0)
-    pl.semaphore_wait(barrier, nz - 1 + n_plane - 1 + more)
+    def keep(slot, p, pt):
+        for n, piece in enumerate(parts_of(p, MOVE[0])):
+            p_b[slot, n] = piece
+        for n, piece in enumerate(parts_of(pt, max(PULL[1], CARRY[1]))):
+            pt_b[slot, n] = piece
+
+    def begin(q):
+        l = layer_at(q, 0)
+        s_ref[q] = inv[l]
+        _, pt = propagator(q, 0)
+        k_ref[q, l] = pt
+        keep(1, *propagator(q, 1))
+
+    def step(q, i):
+        l, before = layer_at(q, i), layer_at(q, i - 1)
+        now, later = lax.rem(i, 2), lax.rem(i + 1, 2)
+        pt = [pt_b[now, n] for n in range(max(PULL[1], CARRY[1]))]
+        p = [p_b[now, n] for n in range(MOVE[0])]
+        y_mat = mm(parts_of(s_ref[q], PULL[0]), pt[: PULL[1]])
+        k_new = mm(parts_of(k_ref[q, before], CARRY[0]), pt[: CARRY[1]])
+        p_next, pt_next = propagator(q, jnp.minimum(i + 1, count - 1))
+        moved = mm(p, parts_of(y_mat, MOVE[1]))
+        keep(later, p_next, pt_next)
+        k_ref[q, l] = k_new
+        s_ref[q] = inv[l] + moved
+        acc[pl.ds(l, 1), :] = acc[pl.ds(l, 1), :] + diagonal(moved)
 
     def halo_up():
         dev = slab_dev(slab + 1)
@@ -185,6 +194,91 @@
     has_up = slab < n_slabs - 1
     has_down = slab > 0
 
+    half = size // 2
+    r_half = lax.broadcasted_iota(jnp.int32, (half, half), 0)
+    c_half = lax.broadcasted_iota(jnp.int32, (half, half), 1)
+
+    def pack(q, mat):
+        one, two = mat[:half, :half], mat[half:, half:]
+        wire_out[q, 0:half] = mat[:half, half:]
+        wire_out[q, half:size] = jnp.where(r_half <= c_half, one, two)
+        line = jnp.sum(jnp.where(r_half == c_half, two, 0.0), axis=0, keepdims=True)
+        wire_out[q, size : size + 8] = jnp.broadcast_to(line, (8, half))
+
+    def unpack(q):
+        side, both = wire_in[q, 0:half], wire_in[q, half:size]
+        over = both.T
+        line = wire_in[q, size : size + 1]
+        e_ref[q, 0:half, half:size] = side
+        e_ref[q, half:size, 0:half] = side.T
+        e_ref[q, 0:half, 0:half] = jnp.where(r_half <= c_half, both, over)
+        two = jnp.where(r_half > c_half, both, over)
+        e_ref[q, half:size, half:size] = jnp.where(r_half == c_half, line, two)
+
+    def relay(q):
+        dev = plane_dev(here + 1 - 2 * q)
+        return pltpu.make_async_remote_copy(
+            wire_out.at[q], wire_in.at[q], relay_send.at[q], relay_recv.at[q], device_id=dev, device_id_type=MESH
+        )
+
+    def row_of(q, eb, l):
+        k_here = k_ref[q, l]
+        g = mm(eb, parts_of(k_here, ENTER[1]))
+        return k_here, g, jnp.sum(g * k_here, axis=0, keepdims=True)
+
+    def add_row(l, row):
+        acc[pl.ds(l, 1), :] = acc[pl.ds(l, 1), :] + row
+
+    def pass_on(q):
+        at_end = layer == (1 - q) * (n_layer - 1)
+        l = layer_at(q, count - 1)
+        k_last, g, row = row_of(q, parts_of(e_ref[q], ENTER[0]), l)
+
+        @pl.when(jnp.logical_not(at_end))
+        def _():
+            pack(q, s_ref[q] + mm(parts_of(k_last.T, LEAVE[0]), parts_of(g, LEAVE[1])))
+            relay(q).start()
+
+        add_row(l, row)
+
+    def rest(q):
+        eb = parts_of(e_ref[q], ENTER[0])
+        found = [row_of(q, eb, layer_at(q, i))[2] for i in range(count - 1)]
+        for i, row in enumerate(found):
+            add_row(layer_at(q, i), row)
+
+    second = 1 - first
+    for i in range(2):
+        l = layer_at(first, i)
+        pltpu.make_async_copy(inv_hbm.at[l], inv.at[l], inv_sem.at[l]).wait()
+    begin(first)
+    for i in range(2, count):
+        l = layer_at(first, i)
+        pltpu.make_async_copy(inv_hbm.at[l], inv.at[l], inv_sem.at[l]).wait()
+    for i in range(count):
+        acc[i : i + 1, :] = diagonal(inv[i])
+
+    def chain_first(i, carry):
+        step(first, i)
+        return carry
+
+    lax.fori_loop(1, count, chain_first, 0)
+
+    more = jnp.where(extra_up, 1, 0) + jnp.where(extra_down, 1, 0)
+    pl.semaphore_wait(barrier, nz - 1 + n_plane - 1 + more)
+    for edge, copy in zip(edges, lead_loads):
+        pl.when(edge)(copy.wait)
+    outer = jnp.logical_or(*edges)
+    inner_seg = jnp.logical_not(outer)
+
+    @pl.when(inner_seg)
+    def _():
+        begin(second)
+        relay(first).wait_recv()
+        unpack(first)
+
+    pass_on(first)
+
     @pl.when(has_up)
     def _():
         for copy in halo_up():
@@ -195,58 +289,34 @@
         for copy in halo_down():
             copy.start()
 
-    def relay(left):
-        out, e = (out_l, e_l) if left else (out_r, e_r)
-        n = 0 if left else 1
-        to = layer + 1 if left else layer - 1
-        dev = plane_dev((y * nxl + xl) * n_layer + to)
-        return pltpu.make_async_remote_copy(
-            out, e, relay_send.at[n], relay_recv.at[n], device_id=dev, device_id_type=MESH
-        )
-
-    def enter(left):
-        s, k, e, out = (s_l, k_l, e_l, out_l) if left else (s_r, k_r, e_r, out_r)
-        lead = lead_l if left else lead_r
-        at_edge = layer == (0 if left else n_layer - 1)
-        at_end = layer == (n_layer - 1 if left else 0)
-
-        @pl.when(at_edge)
-        def _():
-            e[...] = lead[...]
-
-        @pl.when(jnp.logical_not(at_edge))
-        def _():
-            relay(left).wait_recv()
-
-        eb = parts_of(e[...], PIECES)
-        last = count - 1 if left else 0
-        k_last = k[last]
-        g = mm(eb, parts_of(k_last, PIECES))
-        acc[last : last + 1, :] = acc[last : last + 1, :] + jnp.sum(g * k_last, axis=0, keepdims=True)
-
-        @pl.when(jnp.logical_not(at_end))
-        def _():
-            out[...] = s[...] + mm(parts_of(k_last.T, PIECES), parts_of(g, PIECES))
-            relay(left).start()
-
-        for i in range(1, count):
-            l = count - 1 - i if left else i
-            k_here = k[l]
-            g = mm(eb, parts_of(k_here, PIECES))
-            acc[l : l + 1, :] = acc[l : l + 1, :] + jnp.sum(g * k_here, axis=0, keepdims=True)
-
-    @pl.when(layer < n_layer // 2)
-    def _():
-        enter(True)
-        enter(False)
-
-    @pl.when(layer >= n_layer // 2)
-    def _():
-        enter(False)
-        enter(True)
-
+    @pl.when(outer)
+    def _():
+        begin(second)
+
+    def chain_second(i, carry):
+        step(second, i)
+        return carry
+
+    lax.fori_loop(1, count, chain_second, 0)
+
+    @pl.when(outer)
+    def _():
+        rest(first)
+
+    relay(second).wait_recv()
+    unpack(second)
+    pass_on(second)
+
+    @pl.when(inner_seg)
+    def _():
+        rest(first)
+
+    rest(second)
+
+    for copy in own:
+        copy.wait()
     slots = lax.broadcasted_iota(jnp.int32, qw_ref.shape, 1)
-    weight = jnp.sum(jnp.where(slots == slot_ref[0], qw_ref[...], 0.0), axis=1, keepdims=True)
+    weight = jnp.sum(jnp.where(slots == slot_ref[...], qw_ref[...], 0.0), axis=1, keepdims=True)
     part[...] = weight * acc[...]
 
     def z_copies(src, buf, send, recv):
@@ -305,9 +375,6 @@
     for lay in range(1, n_layer):
         mine = jnp.where(layer == lay, gathered[lay], mine)
     dens_out[...] = mine
-
-    for copy in own:
-        copy.wait()
 
     @pl.when(has_down)
     def _():
@@ -456,13 +523,11 @@
     for copy in p_copies(psrc, pbuf, ps, pr) + p_copies(msrc, pmom, mps, mpr):
         copy.wait_send()
 
-    @pl.when(layer < n_layer - 1)
-    def _():
-        relay(True).wait_send()
-
-    @pl.when(layer > 0)
-    def _():
-        relay(False).wait_send()
+    relay(first).wait_send()
+
+    @pl.when(inner_seg)
+    def _():
+        relay(second).wait_send()
 
     @pl.when(has_up)
     def _():
@@ -492,12 +557,15 @@
     planes, n_y, n_z = doping.shape
     n_plane = ny * nxl * nxh * nc
     vmem = pl.BlockSpec(memory_space=pltpu.VMEM)
-    hbm = pl.BlockSpec(memory_space=pl.ANY)
-    smem = pl.BlockSpec(memory_space=pltpu.SMEM)
+    hbm = pl.BlockSpec(memory_space=pltpu.HBM)
     square = pltpu.VMEM((size, size), F32)
     squares = pltpu.VMEM((count, size, size), F32)
     dma = pltpu.SemaphoreType.DMA
     rows = pltpu.VMEM((count, size), F32)
+    operands = (
+        layer_inverse[0], coupling, lead_left[0], lead_right[0], quad_weight[None], energy_slot[None], plane_of[None],
+        doping, screening,
+    )
     return pl.pallas_call(
         functools.partial(kernel, sizes),
         out_shape=(
@@ -505,13 +573,23 @@
             jax.ShapeDtypeStruct(doping.shape, F32),
             jax.ShapeDtypeStruct(doping.shape, F32),
         ),
-        in_specs=[hbm, vmem, vmem, vmem, vmem, smem, vmem, hbm, hbm],
+        in_specs=[hbm] * 9,
         out_specs=(vmem, vmem, vmem),
         scratch_shapes=[
             squares,
-            pltpu.VMEM((PIECES, size, size), BF16),
-            pltpu.VMEM((PIECES, size, size), BF16),
-            square, square, squares, squares, rows, square, square, square, square,
+            square,
+            pltpu.VMEM((2, PROP[1], size, size), BF16),
+            pltpu.VMEM((2, MOVE[0], size, size), BF16),
+            pltpu.VMEM((2, max(PULL[1], CARRY[1]), size, size), BF16),
+            pltpu.VMEM((2, size, size), F32),
+            pltpu.VMEM((2, count, size, size), F32),
+            rows,
+            pltpu.VMEM((2, size, size), F32),
+            pltpu.VMEM((2, size + 8, size // 2), F32),
+            pltpu.VMEM((2, size + 8, size // 2), F32),
+            pltpu.VMEM((1, quad_weight.shape[0]), F32),
+            pltpu.VMEM((1, 1), jnp.int32),
+            pltpu.VMEM((1, plane_of.shape[0]), jnp.int32),
             pltpu.VMEM((planes + 6, n_y, n_z), F32),
             pltpu.VMEM((planes + 4, n_y, n_z), F32),
             pltpu.VMEM((planes + 4, n_y, n_z), F32),
@@ -525,24 +603,14 @@
             pltpu.VMEM((nz, 1, 128), F32),
             pltpu.VMEM((n_plane, 1, 128), F32),
             pltpu.VMEM((1, 128), F32),
-            dma((count,)), dma((2,)), dma((4,)), dma((4,)), dma((2,)), dma((2,)),
+            dma((count,)), dma((8,)), dma((4,)), dma((4,)), dma((2,)), dma((2,)),
             dma((nz,)), dma((nz,)), dma((n_plane,)), dma((n_plane,)),
             dma((nz,)), dma((nz,)), dma((n_plane,)), dma((n_plane,)),
         ],
         compiler_params=pltpu.CompilerParams(
-            collective_id=0, has_side_effects=True, vmem_limit_bytes=48 * 1024 * 1024
+            collective_id=0, has_side_effects=True, vmem_limit_bytes=VMEM
         ),
-    )(
-        layer_inverse[0],
-        coupling,
-        lead_left[0],
-        lead_right[0],
-        quad_weight[None],
-        energy_slot,
-        plane_of[None],
-        doping,
-        screening,
-    )
+    )(*[v if v.size == 1 else pltpu.with_memory_space_constraint(v, pltpu.HBM) for v in operands])
 
 
 def sharded(split):

time: 70.8 us -> 51.2 us (0.72)
  Pallas kernels: 59.6 us -> 47.8 us
  local copies, waits for them, and re-layouts: 9.65 us -> 2.01 us
    pallas_call x1, Pallas kernels: 59.6 us -> 47.8 us  [body(): pl.pallas_call(functools.partial(kernel, sizes), out_shape=(jax.ShapeDtyp...]
    unnamed x19 -> x3, local copies, waits for them, and re-layouts: 9.65 us -> 2.01 us
where the time goes in v1:
time: 51.2 us; the launch traced here: 51.1 us
  Pallas kernels  47.8 us (93%)
  local copies, waits for them, and re-layouts  2.01 us (4%)
  between operations  1.29 us (3%)
    pallas_call x1, Pallas kernels, body(): pl.pallas_call(functools.partial(kernel, sizes), out_shape=(jax.ShapeDtyp...  47.8 us
    unnamed x3, local copies, waits for them, and re-layouts  2.01 us

profile of v1, /device:TPU:1, one launch (start us, length us, event | category | flops | bytes accessed | tf_op | source)
XLA Modules:
  0.0 51.1 jit_solution(259871474679769302)
XLA Ops:
  1.3 47.8 %shard_map.112 = (f32[8,256]{1,0:T(8,128)S(1)}, f32[4,128,128]{2,1,0:T(8,128)S(1)}, f32[4,128,128]{2,1,0:T(8,128)S(1)}) custom-call(f32[8,256,256]{2,1,0:T(8,128)} %bitcast.7, f32[256,256]{1,0:T(8,128)} %t_hbm.1, f32[256,256]{1,0:T(8,128)} %bitcast.8, f32[256,256]{1,0:T(8,128)} %bitcast.9, f32[1,64]{1,0:T(1,128)} %bitcast.10, s32[1,1]{1,0:T(1,128)} %bitcast.6.slot_hbm, ...), custom_call_target="tpu_custom_call" | custom-call | tf_op jit(solution)/shard_map/pallas_call | solution.py:569
  49.0 0.6 %copy.16 = f32[8,256]{1,0:T(8,128)} copy(f32[8,256]{1,0:T(8,128)S(1)} %get-tuple-element.6) | data formatting | bytes 16384
  49.6 0.7 %copy.17 = f32[4,128,128]{2,1,0:T(8,128)} copy(f32[4,128,128]{2,1,0:T(8,128)S(1)} %get-tuple-element.7) | data formatting | bytes 524288
  50.3 0.7 %copy.18 = f32[4,128,128]{2,1,0:T(8,128)} copy(f32[4,128,128]{2,1,0:T(8,128)S(1)} %get-tuple-element.8) | data formatting | bytes 524288

commit v2 on v1

--- a/solution.py
+++ b/solution.py
@@ -15,12 +15,13 @@
 CG_ITERS = 3
 SHIFT = 7.0
 VMEM = 48 * 1024 * 1024
-PROP = (2, 2)
 PULL = (2, 2)
 CARRY = (2, 2)
 MOVE = (2, 2)
 ENTER = (1, 1)
 LEAVE = (1, 1)
+EARLY = 1
+MEET = 4
 MESH = pl.DeviceIdType.MESH
 HI = lax.Precision.HIGHEST
 F32 = jnp.float32
@@ -51,8 +52,8 @@
     sizes,
     inv_hbm, t_hbm, lead_l, lead_r, qw_hbm, slot_hbm, plane_hbm, dop_hbm, scr_hbm,
     dens_out, pot_out, res_out,
-    inv, t_ref, tt, p_b, pt_b, s_ref, k_ref, acc, e_ref, wire_in, wire_out, qw_ref, slot_ref, plane_ref,
-    dopx, scrx, u1, u2, u3, part, zbuf, pbuf, psrc, mom, zmom, pmom, msrc,
+    inv, t_ref, t_both, t_b, s_ref, k_ref, acc, e_ref, wire_in, wire_out, qw_ref, slot_ref, plane_ref,
+    dopx, scrx, u1, u2, u3, part, zbuf, psrc, pbuf, mom, zmom, pmom, msrc,
     inv_sem, own_sem, halo_send, halo_recv, relay_send, relay_recv,
     zs, zr, ps, pr, mzs, mzr, mps, mpr,
 ):
@@ -80,22 +81,6 @@
         en, lay = lax.div(index, n_layer), lax.rem(index, n_layer)
         group, zz = lax.div(en, nz), lax.rem(en, nz)
         return (lax.div(group, nxl), lax.rem(group, nxl), zz, lax.div(lay, nc), lax.rem(lay, nc))
-
-    barrier = pltpu.get_barrier_semaphore()
-    extra_up = jnp.logical_and(layer == n_layer - 1, energy < n_energy - 1)
-    extra_down = jnp.logical_and(layer == 0, energy > 0)
-    for k in range(1, nz):
-        pl.semaphore_signal(barrier, inc=1, device_id=z_dev(lax.rem(z + k, nz)), device_id_type=MESH)
-    for k in range(1, n_plane):
-        pl.semaphore_signal(barrier, inc=1, device_id=plane_dev(lax.rem(here + k, n_plane)), device_id_type=MESH)
-
-    @pl.when(extra_up)
-    def _():
-        pl.semaphore_signal(barrier, inc=1, device_id=slab_dev(slab + 1), device_id_type=MESH)
-
-    @pl.when(extra_down)
-    def _():
-        pl.semaphore_signal(barrier, inc=1, device_id=slab_dev(slab - 1), device_id_type=MESH)
 
     first = jnp.where(layer >= n_layer // 2, 1, 0)
 
@@ -124,11 +109,26 @@
     for copy in own:
         copy.start()
 
+    barrier = pltpu.get_barrier_semaphore()
+    extra_up = jnp.logical_and(layer == n_layer - 1, energy < n_energy - 1)
+    extra_down = jnp.logical_and(layer == 0, energy > 0)
+    for k in range(1, nz):
+        pl.semaphore_signal(barrier, inc=1, device_id=z_dev(lax.rem(z + k, nz)), device_id_type=MESH)
+    for k in range(1, n_plane):
+        pl.semaphore_signal(barrier, inc=1, device_id=plane_dev(lax.rem(here + k, n_plane)), device_id_type=MESH)
+
+    @pl.when(extra_up)
+    def _():
+        pl.semaphore_signal(barrier, inc=1, device_id=slab_dev(slab + 1), device_id_type=MESH)
+
+    @pl.when(extra_down)
+    def _():
+        pl.semaphore_signal(barrier, inc=1, device_id=slab_dev(slab - 1), device_id_type=MESH)
+
     t_load.wait()
-    t = t_ref[...]
-    for n, (piece, across) in enumerate(zip(parts_of(t, PROP[1]), parts_of(t.T, PROP[1]))):
-        tt[0, n] = piece
-        tt[1, n] = across
+    for q, value in enumerate((t_ref[...], t_ref[...].T)):
+        t_both[q] = value
+        t_b[q] = value.astype(BF16)
 
     rows = lax.broadcasted_iota(jnp.int32, (size, size), 0)
     cols = lax.broadcasted_iota(jnp.int32, (size, size), 1)
@@ -137,37 +137,37 @@
         return jnp.sum(jnp.where(rows == cols, mat, 0.0), axis=0, keepdims=True)
 
     def propagator(q, i):
-        d = parts_of(inv[layer_at(q, i)], PROP[0])
-        a = [tt[q, n] for n in range(PROP[1])]
-        b = [tt[1 - q, n] for n in range(PROP[1])]
-        return mm(d, a), mm(b, d)
-
-    def keep(slot, p, pt):
-        for n, piece in enumerate(parts_of(p, MOVE[0])):
-            p_b[slot, n] = piece
-        for n, piece in enumerate(parts_of(pt, max(PULL[1], CARRY[1]))):
-            pt_b[slot, n] = piece
+        d = inv[layer_at(q, i)]
+        on = jnp.where(rows == cols, d, 0.0)
+        down = jnp.sum(on, axis=1, keepdims=True)
+        along = jnp.sum(on, axis=0, keepdims=True)
+        off = [jnp.where(rows == cols, 0.0, d).astype(BF16)]
+        p = down * t_both[q] + mm(off, [t_b[q]])
+        pt = along * t_both[1 - q] + mm([t_b[1 - q]], off)
+        return p, pt
+
+    def pieces(p, pt):
+        return parts_of(p, MOVE[0]), parts_of(pt, max(PULL[1], CARRY[1]))
 
     def begin(q):
         l = layer_at(q, 0)
-        s_ref[q] = inv[l]
-        _, pt = propagator(q, 0)
-        k_ref[q, l] = pt
-        keep(1, *propagator(q, 1))
-
-    def step(q, i):
-        l, before = layer_at(q, i), layer_at(q, i - 1)
-        now, later = lax.rem(i, 2), lax.rem(i + 1, 2)
-        pt = [pt_b[now, n] for n in range(max(PULL[1], CARRY[1]))]
-        p = [p_b[now, n] for n in range(MOVE[0])]
-        y_mat = mm(parts_of(s_ref[q], PULL[0]), pt[: PULL[1]])
-        k_new = mm(parts_of(k_ref[q, before], CARRY[0]), pt[: CARRY[1]])
-        p_next, pt_next = propagator(q, jnp.minimum(i + 1, count - 1))
+        k = propagator(q, 0)[1]
+        k_ref[q, l] = k
+        return inv[l], k, pieces(*propagator(q, 1))
+
+    def step(q, i, chain):
+        s, k, (p, pt) = chain
+        l = layer_at(q, i)
+        y_mat = mm(parts_of(s, PULL[0]), pt[: PULL[1]])
+        k = mm(parts_of(k, CARRY[0]), pt[: CARRY[1]])
+        ahead = pieces(*propagator(q, i + 1)) if i + 1 < count else None
         moved = mm(p, parts_of(y_mat, MOVE[1]))
-        keep(later, p_next, pt_next)
-        k_ref[q, l] = k_new
-        s_ref[q] = inv[l] + moved
+        k_ref[q, l] = k
+        s = inv[l] + moved
         acc[pl.ds(l, 1), :] = acc[pl.ds(l, 1), :] + diagonal(moved)
+        if i + 1 == count:
+            s_ref[q] = s
+        return s, k, ahead
 
     def halo_up():
         dev = slab_dev(slab + 1)
@@ -251,53 +251,54 @@
     for i in range(2):
         l = layer_at(first, i)
         pltpu.make_async_copy(inv_hbm.at[l], inv.at[l], inv_sem.at[l]).wait()
-    begin(first)
+    chain = begin(first)
     for i in range(2, count):
         l = layer_at(first, i)
         pltpu.make_async_copy(inv_hbm.at[l], inv.at[l], inv_sem.at[l]).wait()
     for i in range(count):
         acc[i : i + 1, :] = diagonal(inv[i])
-
-    def chain_first(i, carry):
-        step(first, i)
-        return carry
-
-    lax.fori_loop(1, count, chain_first, 0)
+    outer = jnp.logical_or(*edges)
+    inner_seg = jnp.logical_not(outer)
+
+    def start_halos():
+        @pl.when(has_up)
+        def _():
+            for copy in halo_up():
+                copy.start()
+
+        @pl.when(has_down)
+        def _():
+            for copy in halo_down():
+                copy.start()
+
+    for i in range(1, MEET):
+        chain = step(first, i, chain)
 
     more = jnp.where(extra_up, 1, 0) + jnp.where(extra_down, 1, 0)
     pl.semaphore_wait(barrier, nz - 1 + n_plane - 1 + more)
+    pl.when(outer)(start_halos)
+
+    for i in range(MEET, count):
+        chain = step(first, i, chain)
     for edge, copy in zip(edges, lead_loads):
         pl.when(edge)(copy.wait)
-    outer = jnp.logical_or(*edges)
-    inner_seg = jnp.logical_not(outer)
+
+    @pl.when(outer)
+    def _():
+        pass_on(first)
+
+    chain = begin(second)
+    for i in range(1, 1 + EARLY):
+        chain = step(second, i, chain)
 
     @pl.when(inner_seg)
     def _():
-        begin(second)
         relay(first).wait_recv()
         unpack(first)
-
-    pass_on(first)
-
-    @pl.when(has_up)
-    def _():
-        for copy in halo_up():
-            copy.start()
-
-    @pl.when(has_down)
-    def _():
-        for copy in halo_down():
-            copy.start()
-
-    @pl.when(outer)
-    def _():
-        begin(second)
-
-    def chain_second(i, carry):
-        step(second, i)
-        return carry
-
-    lax.fori_loop(1, count, chain_second, 0)
+        pass_on(first)
+
+    for i in range(1 + EARLY, count):
+        chain = step(second, i, chain)
 
     @pl.when(outer)
     def _():
@@ -309,6 +310,7 @@
 
     @pl.when(inner_seg)
     def _():
+        start_halos()
         rest(first)
 
     rest(second)
@@ -319,57 +321,35 @@
     weight = jnp.sum(jnp.where(slots == slot_ref[...], qw_ref[...], 0.0), axis=1, keepdims=True)
     part[...] = weight * acc[...]
 
-    def z_copies(src, buf, send, recv):
-        done = []
-        for k in range(1, nz):
-            to = lax.rem(z + k, nz)
-            done.append(pltpu.make_async_remote_copy(
-                src, buf.at[z], send.at[to], recv.at[z], device_id=z_dev(to), device_id_type=MESH))
-        return done
-
-    def z_arrivals(src, buf, send, recv):
-        done = []
-        for k in range(1, nz):
-            source = lax.rem(z + k, nz)
-            done.append(pltpu.make_async_remote_copy(
-                src, buf.at[source], send.at[source], recv.at[source], device_id=z_dev(source), device_id_type=MESH))
-        return done
-
-    def p_copies(src, buf, send, recv):
-        done = []
-        for k in range(1, n_plane):
-            to = lax.rem(here + k, n_plane)
-            done.append(pltpu.make_async_remote_copy(
-                src, buf.at[here], send.at[to], recv.at[here], device_id=plane_dev(to), device_id_type=MESH))
-        return done
-
-    def p_arrivals(src, buf, send, recv):
-        done = []
-        for k in range(1, n_plane):
-            source = lax.rem(here + k, n_plane)
-            done.append(pltpu.make_async_remote_copy(
-                src, buf.at[source], send.at[source], recv.at[source], device_id=plane_dev(source), device_id_type=MESH))
-        return done
-
-    def exchange(copies, arrivals, src, buf, mine, send, recv):
-        for copy in copies(src, buf, send, recv):
+    along_z = (nz, z, z_dev)
+    in_plane = (n_plane, here, plane_dev)
+
+    def copies(group, src, buf, send, recv, arriving):
+        number, me, device = group
+        for k in range(1, number):
+            other = lax.rem(me + k, number)
+            slot = other if arriving else me
+            yield pltpu.make_async_remote_copy(
+                src, buf.at[slot], send.at[other], recv.at[slot], device_id=device(other), device_id_type=MESH
+            )
+
+    def exchange(group, src, buf, send, recv):
+        for copy in copies(group, src, buf, send, recv, False):
             copy.start()
-        buf[mine] = src[...]
-        for copy in arrivals(src, buf, send, recv):
+        buf[group[1]] = src[...]
+        for copy in copies(group, src, buf, send, recv, True):
             copy.wait_recv()
 
-    exchange(z_copies, z_arrivals, part, zbuf, z, zs, zr)
-    total = zbuf[0]
-    for k in range(1, nz):
-        total = total + zbuf[k]
-    psrc[...] = total
-    exchange(p_copies, p_arrivals, psrc, pbuf, here, ps, pr)
-    gathered = []
-    for lay in range(n_layer):
-        total = pbuf[lay]
-        for k in range(1, ny * nxl):
-            total = total + pbuf[k * n_layer + lay]
-        gathered.append(total)
+    def total_of(buf, slots):
+        total = None
+        for k in slots:
+            total = buf[k] if total is None else total + buf[k]
+        return total
+
+    exchange(along_z, part, zbuf, zs, zr)
+    psrc[...] = total_of(zbuf, range(nz))
+    exchange(in_plane, psrc, pbuf, ps, pr)
+    gathered = [total_of(pbuf, range(lay, n_plane, n_layer)) for lay in range(n_layer)]
     dens = jnp.concatenate(gathered, axis=0)
     mine = gathered[0]
     for lay in range(1, n_layer):
@@ -458,15 +438,10 @@
     for k, value in enumerate(sums):
         row = jnp.where(lane == k, value, row)
     mom[...] = row
-    exchange(z_copies, z_arrivals, mom, zmom, z, mzs, mzr)
-    total = zmom[0]
-    for k in range(1, nz):
-        total = total + zmom[k]
-    msrc[...] = total
-    exchange(p_copies, p_arrivals, msrc, pmom, here, mps, mpr)
-    total = pmom[0]
-    for k in range(1, n_plane):
-        total = total + pmom[k]
+    exchange(along_z, mom, zmom, mzs, mzr)
+    msrc[...] = total_of(zmom, range(nz))
+    exchange(in_plane, msrc, pmom, mps, mpr)
+    total = total_of(pmom, range(n_plane))
     moment = [total[:, k : k + 1] for k in range(6)]
 
     def product(a, b):
@@ -518,10 +493,12 @@
             r = r + residual[k] * v[k]
         res_out[q] = r
 
-    for copy in z_copies(part, zbuf, zs, zr) + z_copies(mom, zmom, mzs, mzr):
-        copy.wait_send()
-    for copy in p_copies(psrc, pbuf, ps, pr) + p_copies(msrc, pmom, mps, mpr):
-        copy.wait_send()
+    for sent in (
+        (along_z, part, zbuf, zs, zr), (in_plane, psrc, pbuf, ps, pr),
+        (along_z, mom, zmom, mzs, mzr), (in_plane, msrc, pmom, mps, mpr),
+    ):
+        for copy in copies(*sent, False):
+            copy.wait_send()
 
     relay(first).wait_send()
 
@@ -578,9 +555,8 @@
         scratch_shapes=[
             squares,
             square,
-            pltpu.VMEM((2, PROP[1], size, size), BF16),
-            pltpu.VMEM((2, MOVE[0], size, size), BF16),
-            pltpu.VMEM((2, max(PULL[1], CARRY[1]), size, size), BF16),
+            pltpu.VMEM((2, size, size), F32),
+            pltpu.VMEM((2, size, size), BF16),
             pltpu.VMEM((2, size, size), F32),
             pltpu.VMEM((2, count, size, size), F32),
             rows,
@@ -597,8 +573,8 @@
             pltpu.VMEM((planes, n_y, n_z), F32),
             rows,
             pltpu.VMEM((nz, count, size), F32),
+            rows,
             pltpu.VMEM((n_plane, count, size), F32),
-            rows,
             pltpu.VMEM((1, 128), F32),
             pltpu.VMEM((nz, 1, 128), F32),
             pltpu.VMEM((n_plane, 1, 128), F32),

time: 51.2 us -> 48.3 us (0.943)
  Pallas kernels: 47.8 us -> 44.9 us
    pallas_call x1, Pallas kernels: 47.8 us -> 44.9 us  [body(): pl.pallas_call(functools.partial(kernel, sizes), out_shape=(jax.ShapeDtyp...]
where the time goes in v2:
time: 48.3 us; the launch traced here: 48.2 us
  Pallas kernels  44.9 us (93%)
  local copies, waits for them, and re-layouts  2.01 us (4%)
  between operations  1.29 us (3%)
    pallas_call x1, Pallas kernels, body(): pl.pallas_call(functools.partial(kernel, sizes), out_shape=(jax.ShapeDtyp...  44.9 us
    unnamed x3, local copies, waits for them, and re-layouts  2.01 us

profile of v2, /device:TPU:1, one launch (start us, length us, event | category | flops | bytes accessed | tf_op | source)
XLA Modules:
  0.0 48.2 jit_solution(10129275127366230130)
XLA Ops:
  1.3 44.9 %shard_map.112 = (f32[8,256]{1,0:T(8,128)S(1)}, f32[4,128,128]{2,1,0:T(8,128)S(1)}, f32[4,128,128]{2,1,0:T(8,128)S(1)}) custom-call(f32[8,256,256]{2,1,0:T(8,128)} %bitcast.7, f32[256,256]{1,0:T(8,128)} %t_hbm.1, f32[256,256]{1,0:T(8,128)} %bitcast.8, f32[256,256]{1,0:T(8,128)} %bitcast.9, f32[1,64]{1,0:T(1,128)} %bitcast.10, s32[1,1]{1,0:T(1,128)} %bitcast.6.slot_hbm, ...), custom_call_target="tpu_custom_call" | custom-call | tf_op jit(solution)/shard_map/pallas_call | solution.py:546
  46.2 0.6 %copy.16 = f32[8,256]{1,0:T(8,128)} copy(f32[8,256]{1,0:T(8,128)S(1)} %get-tuple-element.6) | data formatting | bytes 16384
  46.8 0.7 %copy.17 = f32[4,128,128]{2,1,0:T(8,128)} copy(f32[4,128,128]{2,1,0:T(8,128)S(1)} %get-tuple-element.7) | data formatting | bytes 524288
  47.5 0.7 %copy.18 = f32[4,128,128]{2,1,0:T(8,128)} copy(f32[4,128,128]{2,1,0:T(8,128)S(1)} %get-tuple-element.8) | data formatting | bytes 524288

commit v3 on v2

--- a/solution.py
+++ b/solution.py
@@ -1,4 +1,5 @@
 import functools
+import itertools
 
 import jax
 import jax.numpy as jnp
@@ -15,13 +16,13 @@
 CG_ITERS = 3
 SHIFT = 7.0
 VMEM = 48 * 1024 * 1024
-PULL = (2, 2)
-CARRY = (2, 2)
-MOVE = (2, 2)
+PULL = (1, 2)
+CARRY = (1, 2)
+MOVE = (2, 1)
 ENTER = (1, 1)
 LEAVE = (1, 1)
 EARLY = 1
-MEET = 4
+MEET = 6
 MESH = pl.DeviceIdType.MESH
 HI = lax.Precision.HIGHEST
 F32 = jnp.float32
@@ -51,7 +52,7 @@
 def kernel(
     sizes,
     inv_hbm, t_hbm, lead_l, lead_r, qw_hbm, slot_hbm, plane_hbm, dop_hbm, scr_hbm,
-    dens_out, pot_out, res_out,
+    dens_out, both_out,
     inv, t_ref, t_both, t_b, s_ref, k_ref, acc, e_ref, wire_in, wire_out, qw_ref, slot_ref, plane_ref,
     dopx, scrx, u1, u2, u3, part, zbuf, psrc, pbuf, mom, zmom, pmom, msrc,
     inv_sem, own_sem, halo_send, halo_recv, relay_send, relay_recv,
@@ -70,17 +71,21 @@
     count, size, _ = inv_hbm.shape
     planes = dop_hbm.shape[0]
 
-    def plane_dev(index):
-        group, lay = lax.div(index, n_layer), lax.rem(index, n_layer)
-        return (lax.div(group, nxl), lax.rem(group, nxl), z, lax.div(lay, nc), lax.rem(lay, nc))
-
-    def z_dev(index):
-        return (y, xl, index, xh, c)
-
-    def slab_dev(index):
-        en, lay = lax.div(index, n_layer), lax.rem(index, n_layer)
-        group, zz = lax.div(en, nz), lax.rem(en, nz)
-        return (lax.div(group, nxl), lax.rem(group, nxl), zz, lax.div(lay, nc), lax.rem(lay, nc))
+    on_y, on_xl, on_z, on_xh, on_c = [
+        [lax.rem(at + k, length) for k in range(length)] for at, length in zip((y, xl, z, xh, c), sizes)
+    ]
+
+    def around(k, length):
+        return min(k, length - k)
+
+    steps = sorted(
+        itertools.product(range(ny), range(nxl), range(nxh), range(nc)),
+        key=lambda k: -(around(k[0], ny) + k[1] + 2 * k[2]),
+    )
+    plane_peers = [
+        (on_y[k[0]], on_xl[k[1]], z, on_xh[k[2]], on_c[k[3]]) for k in steps if any(k)
+    ]
+    line_peers = [(y, xl, on_z[k], xh, c) for k in sorted(range(1, nz), key=lambda k: -around(k, nz))]
 
     first = jnp.where(layer >= n_layer // 2, 1, 0)
 
@@ -109,21 +114,27 @@
     for copy in own:
         copy.start()
 
+    def slab_dev(index):
+        en, lay = lax.div(index, n_layer), lax.rem(index, n_layer)
+        group, zz = lax.div(en, nz), lax.rem(en, nz)
+        return (lax.div(group, nxl), lax.rem(group, nxl), zz, lax.div(lay, nc), lax.rem(lay, nc))
+
+    slab_up = slab_dev(jnp.minimum(slab + 1, n_slabs - 1))
+    slab_down = slab_dev(jnp.maximum(slab - 1, 0))
+
     barrier = pltpu.get_barrier_semaphore()
     extra_up = jnp.logical_and(layer == n_layer - 1, energy < n_energy - 1)
     extra_down = jnp.logical_and(layer == 0, energy > 0)
-    for k in range(1, nz):
-        pl.semaphore_signal(barrier, inc=1, device_id=z_dev(lax.rem(z + k, nz)), device_id_type=MESH)
-    for k in range(1, n_plane):
-        pl.semaphore_signal(barrier, inc=1, device_id=plane_dev(lax.rem(here + k, n_plane)), device_id_type=MESH)
+    for peer in line_peers + plane_peers:
+        pl.semaphore_signal(barrier, inc=1, device_id=peer, device_id_type=MESH)
 
     @pl.when(extra_up)
     def _():
-        pl.semaphore_signal(barrier, inc=1, device_id=slab_dev(slab + 1), device_id_type=MESH)
+        pl.semaphore_signal(barrier, inc=1, device_id=slab_up, device_id_type=MESH)
 
     @pl.when(extra_down)
     def _():
-        pl.semaphore_signal(barrier, inc=1, device_id=slab_dev(slab - 1), device_id_type=MESH)
+        pl.semaphore_signal(barrier, inc=1, device_id=slab_down, device_id_type=MESH)
 
     t_load.wait()
     for q, value in enumerate((t_ref[...], t_ref[...].T)):
@@ -170,7 +181,7 @@
         return s, k, ahead
 
     def halo_up():
-        dev = slab_dev(slab + 1)
+        dev = slab_up
         return [
             pltpu.make_async_remote_copy(
                 dop_hbm.at[pl.ds(planes - 3, 3)], dopx.at[pl.ds(0, 3)],
@@ -181,7 +192,7 @@
         ]
 
     def halo_down():
-        dev = slab_dev(slab - 1)
+        dev = slab_down
         return [
             pltpu.make_async_remote_copy(
                 dop_hbm.at[pl.ds(0, 3)], dopx.at[pl.ds(planes + 3, 3)],
@@ -216,7 +227,8 @@
         e_ref[q, half:size, half:size] = jnp.where(r_half == c_half, line, two)
 
     def relay(q):
-        dev = plane_dev(here + 1 - 2 * q)
+        to = jnp.clip(layer + 1 - 2 * q, 0, n_layer - 1)
+        dev = (y, xl, z, lax.div(to, nc), lax.rem(to, nc))
         return pltpu.make_async_remote_copy(
             wire_out.at[q], wire_in.at[q], relay_send.at[q], relay_recv.at[q], device_id=dev, device_id_type=MESH
         )
@@ -276,7 +288,6 @@
 
     more = jnp.where(extra_up, 1, 0) + jnp.where(extra_down, 1, 0)
     pl.semaphore_wait(barrier, nz - 1 + n_plane - 1 + more)
-    pl.when(outer)(start_halos)
 
     for i in range(MEET, count):
         chain = step(first, i, chain)
@@ -302,6 +313,7 @@
 
     @pl.when(outer)
     def _():
+        start_halos()
         rest(first)
 
     relay(second).wait_recv()
@@ -321,24 +333,23 @@
     weight = jnp.sum(jnp.where(slots == slot_ref[...], qw_ref[...], 0.0), axis=1, keepdims=True)
     part[...] = weight * acc[...]
 
-    along_z = (nz, z, z_dev)
-    in_plane = (n_plane, here, plane_dev)
-
-    def copies(group, src, buf, send, recv, arriving):
-        number, me, device = group
-        for k in range(1, number):
-            other = lax.rem(me + k, number)
-            slot = other if arriving else me
-            yield pltpu.make_async_remote_copy(
-                src, buf.at[slot], send.at[other], recv.at[slot], device_id=device(other), device_id_type=MESH
-            )
+    along_z = (z, line_peers)
+    in_plane = (here, plane_peers)
 
     def exchange(group, src, buf, send, recv):
-        for copy in copies(group, src, buf, send, recv, False):
-            copy.start()
-        buf[group[1]] = src[...]
-        for copy in copies(group, src, buf, send, recv, True):
-            copy.wait_recv()
+        me, peers = group
+        for peer in peers:
+            pltpu.make_async_remote_copy(
+                src, buf.at[me], send, recv, device_id=peer, device_id_type=MESH
+            ).start()
+        buf[me] = src[...]
+        all_of(group, src, buf, send, recv).wait_recv()
+
+    def all_of(group, src, buf, send, recv):
+        most = pl.ds(0, len(group[1]))
+        return pltpu.make_async_remote_copy(
+            buf.at[most], buf.at[most], send, recv, device_id=group[1][0], device_id_type=MESH
+        )
 
     def total_of(buf, slots):
         total = None
@@ -487,18 +498,17 @@
         x = potential[0] * v[0]
         for k in range(1, CG_ITERS):
             x = x + potential[k] * v[k]
-        pot_out[q] = x
+        both_out[0, q] = x
         r = residual[0] * v[0]
         for k in range(1, CG_ITERS + 1):
             r = r + residual[k] * v[k]
-        res_out[q] = r
+        both_out[1, q] = r
 
     for sent in (
         (along_z, part, zbuf, zs, zr), (in_plane, psrc, pbuf, ps, pr),
         (along_z, mom, zmom, mzs, mzr), (in_plane, msrc, pmom, mps, mpr),
     ):
-        for copy in copies(*sent, False):
-            copy.wait_send()
+        all_of(*sent).wait_send()
 
     relay(first).wait_send()
 
@@ -543,15 +553,14 @@
         layer_inverse[0], coupling, lead_left[0], lead_right[0], quad_weight[None], energy_slot[None], plane_of[None],
         doping, screening,
     )
-    return pl.pallas_call(
+    dens, both = pl.pallas_call(
         functools.partial(kernel, sizes),
         out_shape=(
             jax.ShapeDtypeStruct((count, size), F32),
-            jax.ShapeDtypeStruct(doping.shape, F32),
-            jax.ShapeDtypeStruct(doping.shape, F32),
+            jax.ShapeDtypeStruct((2, *doping.shape), F32),
         ),
         in_specs=[hbm] * 9,
-        out_specs=(vmem, vmem, vmem),
+        out_specs=(vmem, vmem),
         scratch_shapes=[
             squares,
             square,
@@ -580,13 +589,13 @@
             pltpu.VMEM((n_plane, 1, 128), F32),
             pltpu.VMEM((1, 128), F32),
             dma((count,)), dma((8,)), dma((4,)), dma((4,)), dma((2,)), dma((2,)),
-            dma((nz,)), dma((nz,)), dma((n_plane,)), dma((n_plane,)),
-            dma((nz,)), dma((nz,)), dma((n_plane,)), dma((n_plane,)),
+            *[dma] * 8,
         ],
         compiler_params=pltpu.CompilerParams(
             collective_id=0, has_side_effects=True, vmem_limit_bytes=VMEM
         ),
     )(*[v if v.size == 1 else pltpu.with_memory_space_constraint(v, pltpu.HBM) for v in operands])
+    return dens, both[0], both[1]
 
 
 def sharded(split):

time: 48.3 us -> 44.6 us (0.923)
  Pallas kernels: 44.9 us -> 41.8 us
  local copies, waits for them, and re-layouts: 2.01 us -> 1.43 us
    pallas_call x1, Pallas kernels: 44.9 us -> 41.8 us  [body(): pl.pallas_call(functools.partial(kernel, sizes), out_shape=(jax.ShapeDtyp...]
    unnamed x3 -> x1, local copies, waits for them, and re-layouts: 2.01 us -> 0.6 us
    squeeze x0 -> x1, local copies, waits for them, and re-layouts: none -> 0.83 us  [body(): return (dens, both[0], both[1])]
where the time goes in v3:
time: 44.6 us; the launch traced here: 44.5 us
  Pallas kernels  41.8 us (94%)
  local copies, waits for them, and re-layouts  1.43 us (3%)
  between operations  1.29 us (3%)
    pallas_call x1, Pallas kernels, body(): pl.pallas_call(functools.partial(kernel, sizes), out_shape=(jax.ShapeDtyp...  41.8 us

profile of v3, /device:TPU:1, one launch (start us, length us, event | category | flops | bytes accessed | tf_op | source)
XLA Modules:
  0.0 44.5 jit_solution(12462767415146719979)
XLA Ops:
  1.3 41.8 %shard_map.112 = (f32[8,256]{1,0:T(8,128)S(1)}, f32[2,4,128,128]{3,2,1,0:T(8,128)S(1)}) custom-call(f32[8,256,256]{2,1,0:T(8,128)} %bitcast.11, f32[256,256]{1,0:T(8,128)} %t_hbm.1, f32[256,256]{1,0:T(8,128)} %bitcast.12, f32[256,256]{1,0:T(8,128)} %bitcast.13, f32[1,64]{1,0:T(1,128)} %bitcast.14, s32[1,1]{1,0:T(1,128)} %bitcast.10.slot_hbm, ...), custom_call_target="tpu_custom_call" | custom-call | tf_op jit(solution)/shard_map/pallas_call | solution.py:556
  43.1 0.8 %slice_bitcast_fusion = (f32[4,128,128]{2,1,0:T(8,128)}, f32[4,128,128]{2,1,0:T(8,128)}) fusion(f32[2,4,128,128]{3,2,1,0:T(8,128)S(1)} %get-tuple-element.6), kind=kLoop, calls=%fused_computation | loop fusion | bytes 1048576 | tf_op jit(solution)/shard_map/squeeze | solution.py:598
  43.9 0.6 %copy.14 = f32[8,256]{1,0:T(8,128)} copy(f32[8,256]{1,0:T(8,128)S(1)} %get-tuple-element.12) | data formatting | bytes 16384

commit v4 on v3

--- a/solution.py
+++ b/solution.py
@@ -22,7 +22,6 @@
 ENTER = (1, 1)
 LEAVE = (1, 1)
 EARLY = 1
-MEET = 6
 MESH = pl.DeviceIdType.MESH
 HI = lax.Precision.HIGHEST
 F32 = jnp.float32
@@ -263,12 +262,31 @@
     for i in range(2):
         l = layer_at(first, i)
         pltpu.make_async_copy(inv_hbm.at[l], inv.at[l], inv_sem.at[l]).wait()
-    chain = begin(first)
-    for i in range(2, count):
-        l = layer_at(first, i)
-        pltpu.make_async_copy(inv_hbm.at[l], inv.at[l], inv_sem.at[l]).wait()
-    for i in range(count):
-        acc[i : i + 1, :] = diagonal(inv[i])
+    def settle():
+        for i in range(2, count):
+            l = layer_at(first, i)
+            pltpu.make_async_copy(inv_hbm.at[l], inv.at[l], inv_sem.at[l]).wait()
+        for i in range(count):
+            acc[i : i + 1, :] = diagonal(inv[i])
+
+    def meet():
+        more = jnp.where(extra_up, 1, 0) + jnp.where(extra_down, 1, 0)
+        pl.semaphore_wait(barrier, nz - 1 + n_plane - 1 + more)
+
+    def known(q):
+        s = e_ref[q]
+        ahead = pieces(*propagator(q, 0))
+        settle()
+        for i in range(count):
+            p, pt = ahead
+            l = layer_at(q, i)
+            y_mat = mm(parts_of(s, PULL[0]), pt[: PULL[1]])
+            ahead = pieces(*propagator(q, i + 1)) if i + 1 < count else None
+            moved = mm(p, parts_of(y_mat, MOVE[1]))
+            add_row(l, diagonal(moved))
+            s = inv[l] + moved
+        return s
+
     outer = jnp.logical_or(*edges)
     inner_seg = jnp.logical_not(outer)
 
@@ -283,20 +301,22 @@
             for copy in halo_down():
                 copy.start()
 
-    for i in range(1, MEET):
-        chain = step(first, i, chain)
-
-    more = jnp.where(extra_up, 1, 0) + jnp.where(extra_down, 1, 0)
-    pl.semaphore_wait(barrier, nz - 1 + n_plane - 1 + more)
-
-    for i in range(MEET, count):
-        chain = step(first, i, chain)
-    for edge, copy in zip(edges, lead_loads):
-        pl.when(edge)(copy.wait)
-
     @pl.when(outer)
     def _():
-        pass_on(first)
+        for edge, copy in zip(edges, lead_loads):
+            pl.when(edge)(copy.wait)
+        state = known(first)
+        meet()
+        pack(first, state)
+        relay(first).start()
+
+    @pl.when(inner_seg)
+    def _():
+        chain = begin(first)
+        settle()
+        for i in range(1, count):
+            chain = step(first, i, chain)
+        meet()
 
     chain = begin(second)
     for i in range(1, 1 + EARLY):
@@ -311,19 +331,15 @@
     for i in range(1 + EARLY, count):
         chain = step(second, i, chain)
 
-    @pl.when(outer)
-    def _():
-        start_halos()
+    start_halos()
+
+    @pl.when(inner_seg)
+    def _():
         rest(first)
 
     relay(second).wait_recv()
     unpack(second)
     pass_on(second)
-
-    @pl.when(inner_seg)
-    def _():
-        start_halos()
-        rest(first)
 
     rest(second)
 

time: 44.6 us -> 44.3 us (level)
  no operation moved by 1% of the time
where the time goes in v4:
time: 44.3 us; the launch traced here: 44.2 us
  Pallas kernels  41.5 us (94%)
  local copies, waits for them, and re-layouts  1.43 us (3%)
  between operations  1.29 us (3%)
    pallas_call x1, Pallas kernels, body(): pl.pallas_call(functools.partial(kernel, sizes), out_shape=(jax.ShapeDtyp...  41.5 us

profile of v4, /device:TPU:1, one launch (start us, length us, event | category | flops | bytes accessed | tf_op | source)
XLA Modules:
  0.0 44.2 jit_solution(2905112438347240453)
XLA Ops:
  1.3 41.5 %shard_map.112 = (f32[8,256]{1,0:T(8,128)S(1)}, f32[2,4,128,128]{3,2,1,0:T(8,128)S(1)}) custom-call(f32[8,256,256]{2,1,0:T(8,128)} %bitcast.11, f32[256,256]{1,0:T(8,128)} %t_hbm.1, f32[256,256]{1,0:T(8,128)} %bitcast.12, f32[256,256]{1,0:T(8,128)} %bitcast.13, f32[1,64]{1,0:T(1,128)} %bitcast.14, s32[1,1]{1,0:T(1,128)} %bitcast.10.slot_hbm, ...), custom_call_target="tpu_custom_call" | custom-call | tf_op jit(solution)/shard_map/pallas_call | solution.py:572
  42.8 0.8 %slice_bitcast_fusion = (f32[4,128,128]{2,1,0:T(8,128)}, f32[4,128,128]{2,1,0:T(8,128)}) fusion(f32[2,4,128,128]{3,2,1,0:T(8,128)S(1)} %get-tuple-element.6), kind=kLoop, calls=%fused_computation | loop fusion | bytes 1048576 | tf_op jit(solution)/shard_map/squeeze | solution.py:614
  43.6 0.6 %copy.14 = f32[8,256]{1,0:T(8,128)} copy(f32[8,256]{1,0:T(8,128)S(1)} %get-tuple-element.12) | data formatting | bytes 16384

commit v5 on v4

--- a/solution.py
+++ b/solution.py
@@ -53,9 +53,9 @@
     inv_hbm, t_hbm, lead_l, lead_r, qw_hbm, slot_hbm, plane_hbm, dop_hbm, scr_hbm,
     dens_out, both_out,
     inv, t_ref, t_both, t_b, s_ref, k_ref, acc, e_ref, wire_in, wire_out, qw_ref, slot_ref, plane_ref,
-    dopx, scrx, u1, u2, u3, part, zbuf, psrc, pbuf, mom, zmom, pmom, msrc,
+    dopx, scrx, u1, u2, u3, part, zbuf, psrc, pbuf, mom, amom,
     inv_sem, own_sem, halo_send, halo_recv, relay_send, relay_recv,
-    zs, zr, ps, pr, mzs, mzr, mps, mpr,
+    zs, zr, ps, pr, mas, mar,
 ):
     ny, nxl, nz, nxh, nc = sizes
     y, xl, z, xh, c = [lax.axis_index(a) for a in AXES]
@@ -113,6 +113,12 @@
     for copy in own:
         copy.start()
 
+    everywhere = sorted(
+        itertools.product(range(ny), range(nxl), range(nz), range(nxh), range(nc)),
+        key=lambda k: -(around(k[0], ny) + k[1] + around(k[2], nz) + 2 * k[3]),
+    )
+    all_peers = [(on_y[k[0]], on_xl[k[1]], on_z[k[2]], on_xh[k[3]], on_c[k[4]]) for k in everywhere if any(k)]
+
     def slab_dev(index):
         en, lay = lax.div(index, n_layer), lax.rem(index, n_layer)
         group, zz = lax.div(en, nz), lax.rem(en, nz)
@@ -351,6 +357,7 @@
 
     along_z = (z, line_peers)
     in_plane = (here, plane_peers)
+    over_all = (slab, all_peers)
 
     def exchange(group, src, buf, send, recv):
         me, peers = group
@@ -465,10 +472,9 @@
     for k, value in enumerate(sums):
         row = jnp.where(lane == k, value, row)
     mom[...] = row
-    exchange(along_z, mom, zmom, mzs, mzr)
-    msrc[...] = total_of(zmom, range(nz))
-    exchange(in_plane, msrc, pmom, mps, mpr)
-    total = total_of(pmom, range(n_plane))
+    exchange(over_all, mom, amom, mas, mar)
+    totals = [total_of(amom, range(k, n_slabs, 8)) for k in range(8)]
+    total = sum(totals[1:], totals[0])
     moment = [total[:, k : k + 1] for k in range(6)]
 
     def product(a, b):
@@ -522,7 +528,7 @@
 
     for sent in (
         (along_z, part, zbuf, zs, zr), (in_plane, psrc, pbuf, ps, pr),
-        (along_z, mom, zmom, mzs, mzr), (in_plane, msrc, pmom, mps, mpr),
+        (over_all, mom, amom, mas, mar),
     ):
         all_of(*sent).wait_send()
 
@@ -601,11 +607,9 @@
             rows,
             pltpu.VMEM((n_plane, count, size), F32),
             pltpu.VMEM((1, 128), F32),
-            pltpu.VMEM((nz, 1, 128), F32),
-            pltpu.VMEM((n_plane, 1, 128), F32),
-            pltpu.VMEM((1, 128), F32),
+            pltpu.VMEM((n_plane * nz, 1, 128), F32),
             dma((count,)), dma((8,)), dma((4,)), dma((4,)), dma((2,)), dma((2,)),
-            *[dma] * 8,
+            *[dma] * 6,
         ],
         compiler_params=pltpu.CompilerParams(
             collective_id=0, has_side_effects=True, vmem_limit_bytes=VMEM

time: 44.3 us -> 42.4 us (0.957)
  Pallas kernels: 41.5 us -> 39.6 us
    pallas_call x1, Pallas kernels: 41.5 us -> 39.6 us  [body(): pl.pallas_call(functools.partial(kernel, sizes), out_shape=(jax.ShapeDtyp...]
where the time goes in v5:
time: 42.4 us; the launch traced here: 42.3 us
  Pallas kernels  39.6 us (93%)
  local copies, waits for them, and re-layouts  1.43 us (3%)
  between operations  1.29 us (3%)
    pallas_call x1, Pallas kernels, body(): pl.pallas_call(functools.partial(kernel, sizes), out_shape=(jax.ShapeDtyp...  39.6 us

profile of v5, /device:TPU:1, one launch (start us, length us, event | category | flops | bytes accessed | tf_op | source)
XLA Modules:
  0.0 42.3 jit_solution(16250916732584993258)
XLA Ops:
  1.3 39.6 %shard_map.112 = (f32[8,256]{1,0:T(8,128)S(1)}, f32[2,4,128,128]{3,2,1,0:T(8,128)S(1)}) custom-call(f32[8,256,256]{2,1,0:T(8,128)} %bitcast.11, f32[256,256]{1,0:T(8,128)} %t_hbm.1, f32[256,256]{1,0:T(8,128)} %bitcast.12, f32[256,256]{1,0:T(8,128)} %bitcast.13, f32[1,64]{1,0:T(1,128)} %bitcast.14, s32[1,1]{1,0:T(1,128)} %bitcast.10.slot_hbm, ...), custom_call_target="tpu_custom_call" | custom-call | tf_op jit(solution)/shard_map/pallas_call | solution.py:578
  40.9 0.8 %slice_bitcast_fusion = (f32[4,128,128]{2,1,0:T(8,128)}, f32[4,128,128]{2,1,0:T(8,128)}) fusion(f32[2,4,128,128]{3,2,1,0:T(8,128)S(1)} %get-tuple-element.6), kind=kLoop, calls=%fused_computation | loop fusion | bytes 1048576 | tf_op jit(solution)/shard_map/squeeze | solution.py:618
  41.7 0.6 %copy.14 = f32[8,256]{1,0:T(8,128)} copy(f32[8,256]{1,0:T(8,128)S(1)} %get-tuple-element.12) | data formatting | bytes 16384

commit v6 on v5

--- a/solution.py
+++ b/solution.py
@@ -52,7 +52,7 @@
     sizes,
     inv_hbm, t_hbm, lead_l, lead_r, qw_hbm, slot_hbm, plane_hbm, dop_hbm, scr_hbm,
     dens_out, both_out,
-    inv, t_ref, t_both, t_b, s_ref, k_ref, acc, e_ref, wire_in, wire_out, qw_ref, slot_ref, plane_ref,
+    inv, t_ref, t_both, t_b, s_ref, k_ref, acc, e_ref, wire_in, wire_out, qw_ref, slot_ref, plane_ref, onehot_ref, spread_ref,
     dopx, scrx, u1, u2, u3, part, zbuf, psrc, pbuf, mom, amom,
     inv_sem, own_sem, halo_send, halo_recv, relay_send, relay_recv,
     zs, zr, ps, pr, mas, mar,
@@ -343,16 +343,29 @@
     def _():
         rest(first)
 
-    relay(second).wait_recv()
-    unpack(second)
-    pass_on(second)
-
-    rest(second)
-
     for copy in own:
         copy.wait()
     slots = lax.broadcasted_iota(jnp.int32, qw_ref.shape, 1)
     weight = jnp.sum(jnp.where(slots == slot_ref[...], qw_ref[...], 0.0), axis=1, keepdims=True)
+    low = slab * planes - 3
+    n_near = planes + 6
+    near = 16
+    ids = low + lax.broadcasted_iota(jnp.int32, (near, plane_ref.shape[1]), 0)
+    onehot_ref[...] = jnp.where(plane_ref[...] == ids, 1.0, 0.0)
+    n_side = dop_hbm.shape[2]
+    cell = n_side // ORB
+    spread_m = lax.broadcasted_iota(jnp.int32, (size, n_side), 0)
+    spread_z = lax.broadcasted_iota(jnp.int32, (size, n_side), 1)
+    spread_ref[...] = jnp.where(lax.rem(spread_m, ORB) == lax.div(spread_z, cell), 1.0, 0.0)
+    row_j = lax.broadcasted_iota(jnp.int32, (ORB, size), 0)
+    row_m = lax.broadcasted_iota(jnp.int32, (ORB, size), 1)
+    own_row = row_j == lax.div(row_m, ORB)
+    relay(second).wait_recv()
+    unpack(second)
+    pass_on(second)
+
+    rest(second)
+
     part[...] = weight * acc[...]
 
     along_z = (z, line_peers)
@@ -410,22 +423,9 @@
         dopx[planes + 3 : planes + 6] = jnp.zeros((3, *dopx.shape[1:]), F32)
         scrx[planes + 2 : planes + 4] = jnp.zeros((2, *scrx.shape[1:]), F32)
 
-    low = slab * planes - 3
-    n_near = planes + 6
-    near = 16
-    ids = low + lax.broadcasted_iota(jnp.int32, (near, plane_ref.shape[1]), 0)
-    onehot = jnp.where(plane_ref[...] == ids, 1.0, 0.0)
-    pc = jnp.dot(onehot, dens, precision=HI, preferred_element_type=F32)
-    n_side = dop_hbm.shape[2]
-    cell = n_side // ORB
-    spread_m = lax.broadcasted_iota(jnp.int32, (size, n_side), 0)
-    spread_z = lax.broadcasted_iota(jnp.int32, (size, n_side), 1)
-    spread = jnp.where(lax.rem(spread_m, ORB) == lax.div(spread_z, cell), 1.0, 0.0)
-    row_j = lax.broadcasted_iota(jnp.int32, (ORB, size), 0)
-    row_m = lax.broadcasted_iota(jnp.int32, (ORB, size), 1)
-    own_row = row_j == lax.div(row_m, ORB)
+    pc = jnp.dot(onehot_ref[...], dens, precision=HI, preferred_element_type=F32)
     tall = jnp.concatenate([jnp.where(own_row, pc[q : q + 1, :], 0.0) for q in range(n_near)], axis=0)
-    wide = jnp.dot(tall, spread, precision=HI, preferred_element_type=F32)
+    wide = jnp.dot(tall, spread_ref[...], precision=HI, preferred_element_type=F32)
     n_y = dop_hbm.shape[1]
     for q in range(n_near):
         for j in range(ORB):
@@ -597,6 +597,8 @@
             pltpu.VMEM((1, quad_weight.shape[0]), F32),
             pltpu.VMEM((1, 1), jnp.int32),
             pltpu.VMEM((1, plane_of.shape[0]), jnp.int32),
+            pltpu.VMEM((16, plane_of.shape[0]), F32),
+            pltpu.VMEM((size, n_z), F32),
             pltpu.VMEM((planes + 6, n_y, n_z), F32),
             pltpu.VMEM((planes + 4, n_y, n_z), F32),
             pltpu.VMEM((planes + 4, n_y, n_z), F32),

time: 42.4 us -> 42.4 us (level)
  no operation moved by 1% of the time
where the time goes in v6:
time: 42.4 us; the launch traced here: 42.3 us
  Pallas kernels  39.6 us (93%)
  local copies, waits for them, and re-layouts  1.43 us (3%)
  between operations  1.29 us (3%)
    pallas_call x1, Pallas kernels, body(): pl.pallas_call(functools.partial(kernel, sizes), out_shape=(jax.ShapeDtyp...  39.6 us

profile of v6, /device:TPU:1, one launch (start us, length us, event | category | flops | bytes accessed | tf_op | source)
XLA Modules:
  0.0 42.3 jit_solution(7664879101219731515)
XLA Ops:
  1.3 39.6 %shard_map.112 = (f32[8,256]{1,0:T(8,128)S(1)}, f32[2,4,128,128]{3,2,1,0:T(8,128)S(1)}) custom-call(f32[8,256,256]{2,1,0:T(8,128)} %bitcast.11, f32[256,256]{1,0:T(8,128)} %t_hbm.1, f32[256,256]{1,0:T(8,128)} %bitcast.12, f32[256,256]{1,0:T(8,128)} %bitcast.13, f32[1,64]{1,0:T(1,128)} %bitcast.14, s32[1,1]{1,0:T(1,128)} %bitcast.10.slot_hbm, ...), custom_call_target="tpu_custom_call" | custom-call | tf_op jit(solution)/shard_map/pallas_call | solution.py:578
  40.9 0.8 %slice_bitcast_fusion = (f32[4,128,128]{2,1,0:T(8,128)}, f32[4,128,128]{2,1,0:T(8,128)}) fusion(f32[2,4,128,128]{3,2,1,0:T(8,128)S(1)} %get-tuple-element.6), kind=kLoop, calls=%fused_computation | loop fusion | bytes 1048576 | tf_op jit(solution)/shard_map/squeeze | solution.py:620
  41.7 0.6 %copy.14 = f32[8,256]{1,0:T(8,128)} copy(f32[8,256]{1,0:T(8,128)S(1)} %get-tuple-element.12) | data formatting | bytes 16384
